TPU v7x, 32 devices: a whole 2x2x4 slice. The times are simulated.
32 devices in a mesh: section: 2 (over core), vocab: 16 (over z, y, x).
Axes of the slice: x: 2, y: 2, z: 4, core: 2. Of those that a mesh axis runs over, the one named last changes fastest.
Arguments:
- hidden_in: bfloat16 [2, 256, 7168], P(None, ('section', 'vocab')), may hold values from -6 to 6
- gain_ffn: float32 [7168], replicated, may hold values from 0.4 to 1.6
- w_gate: bfloat16 [7168, 18432], P(None, ('section', 'vocab')), may hold values from -0.0625 to 0.0625
- w_up: bfloat16 [7168, 18432], P(None, ('section', 'vocab')), may hold values from -0.0625 to 0.0625
- w_down: bfloat16 [18432, 7168], P(('section', 'vocab')), may hold values from -0.046875 to 0.046875
- gain_final: float32 [7168], replicated, may hold values from 0.4 to 1.6
- head_weight: bfloat16 [7168, 129280], P(None, ('section', 'vocab')), may hold values from -4.5 to 4.5
- sampled_ids: int32 [2, 256], replicated, may hold values from 0 to 129279
- seq_ids: int32 [2, 256], P(None, ('section', 'vocab')), may hold values from 0 to 7, never falling along the last dimension, each value on 1 to 128 neighbouring positions
Outputs:
- token_logprob: float32 [2, 256], P(None, ('section', 'vocab'))
- log_norm: float32 [2, 256], P(None, ('section', 'vocab'))
- top_mass: float32 [2, 256], P(None, ('section', 'vocab'))
- seq_logprob: float32 [2, 8], replicated
All inputs are finite; a program needn't handle non-finite values.
Results may differ from a plain program's by a relative error of at most 0.006.
Values may be sent and summed in bfloat16 or wider, within the bound.
No kernel may reach another device: no remote copies, remote signals or barrier semaphores. Data moves between devices by JAX's collectives and lax.ppermute only.
A program may use at most 192 MiB of HBM per device.

v0:
```python
import functools

import jax
import jax.numpy as jnp
from jax import lax
from jax.experimental import pallas as pl
from jax.experimental.pallas import tpu as pltpu
from jax.sharding import PartitionSpec as P


SEQS = 8
TOPK = 20
LANES = 128
NET = 32
FFN_VMEM = 40 << 20
HEAD_VMEM = 40 << 20
AXES = ("section", "vocab")
epsilon = 1e-06


def rms_norm(wide, gain):
    square_mean = jnp.mean(wide * wide, axis=-1, keepdims=True)
    return (wide * lax.rsqrt(square_mean + epsilon) * gain).astype(jnp.bfloat16)


def close_kernel(own_ref, kept_ref, came_ref, gain_ref, out_ref):
    branch = kept_ref[...].astype(jnp.float32) + came_ref[...].astype(jnp.float32)
    residual = (own_ref[0].astype(jnp.float32) + branch).astype(jnp.bfloat16)
    out_ref[...] = rms_norm(residual.astype(jnp.float32), gain_ref[...])


def close_block(hidden_in, m, kept, came, gain):
    _, each, width = hidden_in.shape
    whole = pl.BlockSpec((each, width), lambda i: (0, 0))
    return pl.pallas_call(
        close_kernel,
        grid=(1,),
        in_specs=[
            pl.BlockSpec((1, each, width), lambda i: (m, 0, 0)),
            whole,
            whole,
            pl.BlockSpec((1, width), lambda i: (0, 0)),
        ],
        out_specs=whole,
        out_shape=jax.ShapeDtypeStruct((each, width), jnp.bfloat16),
        compiler_params=pltpu.CompilerParams(vmem_limit_bytes=4 << 20),
        cost_estimate=pl.CostEstimate(flops=8 * each * width, bytes_accessed=8 * each * width, transcendentals=0),
        name="close",
    )(hidden_in, kept, came, gain.reshape(1, width))


def step_masks(size):
    bits = [1 << b for b in reversed(range(size.bit_length() - 1))]
    return bits, bits[:-2] + [bits[-1], bits[-2]]


def step_perms(size):
    first, second = step_masks(size)
    return [
        [(s * size + i, s * size + (i ^ mask)) for s, mask in enumerate(pair) for i in range(size)]
        for pair in zip(first, second)
    ]


def core_perm(size):
    return [(s * size + i, (1 - s) * size + i) for s in range(2) for i in range(size)]


def move(rows, perm):
    return lax.ppermute(rows, AXES, perm)


def gather_rows(rows, size):
    held = rows
    for perm in step_perms(size):
        held = jnp.concatenate([held, move(held, perm)], axis=0)
    return held, move(held, core_perm(size))


def scatter_sum(near, far, size):
    held = near + move(far, core_perm(size))
    perms = step_perms(size)
    for j in reversed(range(1, len(perms))):
        half = held.shape[0] // 2
        held = held[:half] + move(held[half:], perms[j])
    half = held.shape[0] // 2
    return held[:half], move(held[half:], perms[0])


def block_owner(size, section, place):
    tables = []
    for masks in step_masks(size):
        table = []
        for q in range(size):
            mask = 0
            for j, m in enumerate(masks):
                if q >> j & 1:
                    mask ^= m
            table.append(mask)
        tables.append(jnp.array(table, jnp.int32))
    mine = jnp.where(section == 0, tables[0], tables[1])
    other = jnp.where(section == 0, tables[1], tables[0])
    return jnp.concatenate([section * size + (place ^ mine), (1 - section) * size + (place ^ other)])


def turned_dot(a, b):
    return lax.dot_general(a, b, (((1,), (1,)), ((), ())), preferred_element_type=jnp.float32)


def ffn_kernel(near_ref, far_ref, wg_ref, wu_ref, wd_ref, near_out, far_out, x_ref, turned_ref, h_ref, *, steps):
    i = pl.program_id(0)
    half = near_ref.shape[0]
    tile = wg_ref.shape[0]

    @pl.when(i == 0)
    def _():
        x_ref[:half] = near_ref[...]
        x_ref[half:] = far_ref[...]

    @pl.when(i < steps)
    def _():
        gate = turned_dot(wg_ref[...], x_ref[...])
        up = turned_dot(wu_ref[...], x_ref[...])
        turned_ref[pl.ds(pl.multiple_of(i * tile, tile), tile), :] = gate / (1.0 + jnp.exp(-gate)) * up

    @pl.when(i == steps - 1)
    def _():
        h_ref[...] = turned_ref[...].T.astype(jnp.bfloat16)

    @pl.when(i >= steps)
    def _():
        part = jnp.dot(h_ref[...], wd_ref[...], preferred_element_type=jnp.float32).astype(near_out.dtype)
        near_out[...] = part[:half]
        far_out[...] = part[half:]


def ffn(near, far, w_gate, w_up, w_down):
    half, width = near.shape
    rows = 2 * half
    hidden = w_gate.shape[1]
    tile = hidden // 2 if hidden % 32 == 0 else hidden
    block = 1792 if width % 1792 == 0 else width
    steps = hidden // tile

    def first(i):
        return jnp.minimum(i, steps - 1)

    def second(i):
        return jnp.maximum(i - steps, 0)

    part = jax.ShapeDtypeStruct((half, width), jnp.bfloat16)
    return pl.pallas_call(
        functools.partial(ffn_kernel, steps=steps),
        grid=(steps + width // block,),
        in_specs=[
            pl.BlockSpec((half, width), lambda i: (0, 0), pipeline_mode=pl.Buffered(1)),
            pl.BlockSpec((half, width), lambda i: (0, 0), pipeline_mode=pl.Buffered(1)),
            pl.BlockSpec((tile, width), lambda i: (first(i), 0)),
            pl.BlockSpec((tile, width), lambda i: (first(i), 0)),
            pl.BlockSpec((hidden, block), lambda i: (0, second(i))),
        ],
        out_specs=[pl.BlockSpec((half, block), lambda i: (0, second(i)))] * 2,
        out_shape=(part, part),
        scratch_shapes=[
            pltpu.VMEM((rows, width), jnp.bfloat16),
            pltpu.VMEM((hidden, rows), jnp.float32),
            pltpu.VMEM((rows, hidden), jnp.bfloat16),
        ],
        cost_estimate=pl.CostEstimate(
            flops=6 * rows * width * hidden, bytes_accessed=2 * width * (3 * hidden + 2 * rows), transcendentals=0
        ),
        compiler_params=pltpu.CompilerParams(vmem_limit_bytes=FFN_VMEM),
        name="ffn",
    )(near, far, w_gate.T, w_up.T, w_down)


def pair(values, i, j):
    a, b = values[i], values[j]
    if b is None:
        return
    if a is None:
        values[i], values[j] = b, None
    else:
        values[i], values[j] = jnp.maximum(a, b), jnp.minimum(a, b)


def sort_net(values):
    values = list(values) + [None] * (NET - len(values))
    p = 1
    while p < NET:
        k = p
        while k >= 1:
            for j in range(k % p, NET - k, 2 * k):
                for i in range(min(k, NET - j - k)):
                    if (i + j) // (2 * p) == (i + j + k) // (2 * p):
                        pair(values, i + j, i + j + k)
            k //= 2
        p *= 2
    return values[:TOPK]


def merge_net(a, b):
    a = list(a) + [None] * (NET - len(a))
    b = list(b) + [None] * (NET - len(b))
    c = []
    for x, y in zip(a, reversed(b)):
        c.append(y if x is None else x if y is None else jnp.maximum(x, y))
    k = NET // 2
    while k >= 1:
        for base in range(0, NET, 2 * k):
            for i in range(base, base + k):
                pair(c, i, i + k)
        k //= 2
    return c[:TOPK]


def head_kernel(
    owner_ref, near_ref, far_ref, w_ref, ids_ref, seq_ref, out_ref, x_ref, logits_ref, stat_ref, table_ref, pack_ref,
    *, steps, width, each
):
    i = pl.program_id(0)
    half = near_ref.shape[0]
    tile = w_ref.shape[0]

    @pl.when(i == 0)
    def _():
        x_ref[:half] = near_ref[...]
        x_ref[half:] = far_ref[...]

    logits_ref[pl.ds(pl.multiple_of(i * tile, tile), tile), :] = turned_dot(w_ref[...], x_ref[...])

    @pl.when(i == steps - 1)
    def _():
        rows = x_ref.shape[0]
        groups = rows // LANES
        whole = width // (8 * NET)
        sub = lax.broadcasted_iota(jnp.int32, (8, LANES), 0)

        def load(start, lanes):
            return logits_ref[pl.ds(start, 8), lanes]

        def rest(lanes):
            values = []
            for start in range(whole * 8 * NET, width, 8):
                value = load(start, lanes)
                if start + 8 > width:
                    value = jnp.where(sub < width - start, value, -jnp.inf)
                values.append(value)
            return values

        stat_ref[...] = jnp.zeros_like(stat_ref)
        for lane in range(0, rows, LANES):
            lanes = slice(lane, lane + LANES)

            def collect(g, best):
                start = pl.multiple_of(g * 8 * NET, 8 * NET)
                return tuple(merge_net(best, sort_net([load(start + 8 * j, lanes) for j in range(NET)])))

            low = jnp.full((8, LANES), -jnp.inf, jnp.float32)
            best = list(lax.fori_loop(0, whole, collect, (low,) * TOPK))
            tail = rest(lanes)
            if tail:
                ranked = sort_net(tail)
                best = merge_net(best, [r for r in ranked if r is not None])
            for shift in (4, 2, 1):
                best = merge_net(best, [pltpu.roll(b, shift, 0) for b in best])
            peak = best[0]
            wanted = jnp.broadcast_to(ids_ref[:, lanes], (8, LANES)) - sub

            def scan(value, start, total, found):
                total = total + jnp.exp(value - peak)
                return total, found + jnp.where(wanted == start, value, 0.0)

            def sweep(g, carry):
                start = pl.multiple_of(g * 8 * NET, 8 * NET)
                totals, founds = list(carry[:4]), list(carry[4:])
                for j in range(NET):
                    t, f = scan(load(start + 8 * j, lanes), start + 8 * j, totals[j % 4], founds[j % 4])
                    totals[j % 4], founds[j % 4] = t, f
                return tuple(totals) + tuple(founds)

            zero = jnp.zeros((8, LANES), jnp.float32)
            carry = list(lax.fori_loop(0, whole, sweep, (zero,) * 8))
            for j, value in enumerate(tail):
                start = whole * 8 * NET + 8 * j
                total = carry[j % 4] + jnp.exp(value - peak)
                hit = wanted == start
                if start + 8 > width:
                    hit = hit & (sub < width - start)
                carry[j % 4], carry[4 + j % 4] = total, carry[4 + j % 4] + jnp.where(hit, value, 0.0)
            total = carry[0] + carry[1] + carry[2] + carry[3]
            found = carry[4] + carry[5] + carry[6] + carry[7]
            for k in range(TOPK):
                stat_ref[k : k + 1, :] = best[k][:1]
            stat_ref[TOPK : TOPK + 1, :] = jnp.sum(total, axis=0, keepdims=True)
            stat_ref[TOPK + 1 : TOPK + 2, :] = jnp.sum(found, axis=0, keepdims=True)
            turned = stat_ref[...].T
            for j in range(LANES // each):
                owner = owner_ref[lane // each + j]
                block = turned[j * each : (j + 1) * each]
                out_ref[owner, :each, :] = block
                start = owner * each if each % 8 else pl.multiple_of(owner * each, 8)
                table_ref[pl.ds(start, each), :] = block
        for g in range(groups):
            turned = table_ref[g * LANES : (g + 1) * LANES, :].T
            for k, entry in enumerate((0, TOPK, TOPK + 1)):
                pack_ref[k * groups + g : k * groups + g + 1, :] = turned[entry : entry + 1]
            pack_ref[3 * groups + g : 3 * groups + g + 1, :] = seq_ref[g : g + 1, :]
        out_ref[:, each:, :] = jnp.broadcast_to(pack_ref[...][None], (out_ref.shape[0],) + pack_ref.shape)


def head(owner, near, far, w, ids, seq, tile=680):
    half, depth = near.shape
    rows = 2 * half
    width = w.shape[1]
    devices = owner.shape[0]
    each = rows // devices
    groups = rows // LANES
    packed = -(-4 * groups // 8) * 8
    steps = -(-width // tile)
    return pl.pallas_call(
        functools.partial(head_kernel, steps=steps, width=width, each=each),
        grid_spec=pltpu.PrefetchScalarGridSpec(
            num_scalar_prefetch=1,
            grid=(steps,),
            in_specs=[
                pl.BlockSpec((half, depth), lambda i, o: (0, 0), pipeline_mode=pl.Buffered(1)),
                pl.BlockSpec((half, depth), lambda i, o: (0, 0), pipeline_mode=pl.Buffered(1)),
                pl.BlockSpec((tile, depth), lambda i, o: (i, 0)),
                pl.BlockSpec((1, rows), lambda i, o: (0, 0)),
                pl.BlockSpec((groups, LANES), lambda i, o: (0, 0)),
            ],
            out_specs=pl.BlockSpec((devices, each + packed, LANES), lambda i, o: (0, 0, 0)),
            scratch_shapes=[
                pltpu.VMEM((rows, depth), jnp.bfloat16),
                pltpu.VMEM((steps * tile, rows), jnp.float32),
                pltpu.VMEM((LANES, LANES), jnp.float32),
                pltpu.VMEM((rows, LANES), jnp.float32),
                pltpu.VMEM((packed, LANES), jnp.float32),
            ],
        ),
        out_shape=jax.ShapeDtypeStruct((devices, each + packed, LANES), jnp.float32),
        cost_estimate=pl.CostEstimate(
            flops=2 * rows * depth * width, bytes_accessed=2 * depth * (width + rows), transcendentals=rows * width
        ),
        compiler_params=pltpu.CompilerParams(vmem_limit_bytes=HEAD_VMEM),
        name="head",
    )(owner, near, far, w.T, ids, seq)


def finish_kernel(*refs, batches, each, groups):
    stats, (lp_ref, norm_ref, mass_ref, seq_out) = refs[:batches], refs[batches:]
    sources = stats[0].shape[0]
    lane = lax.broadcasted_iota(jnp.int32, (each, LANES), 1)
    row = lax.broadcasted_iota(jnp.int32, (each, LANES), 0)
    seq_row = lax.broadcasted_iota(jnp.int32, (SEQS, LANES), 0).astype(jnp.float32)
    seq_lane = lax.broadcasted_iota(jnp.int32, (SEQS, LANES), 1)
    seq_place = lax.broadcasted_iota(jnp.int32, (SEQS, LANES), 0)

    def across(column):
        return jnp.sum(jnp.where(lane == row, column, 0.0), axis=0, keepdims=True)

    for m in range(batches):
        values = [stats[m][s, :each] for s in range(sources)]
        pool = [jnp.where(lane < TOPK, v, -jnp.inf) for v in values]
        best = pool[0]
        for v in pool[1:]:
            best = jnp.maximum(best, v)
        peak = jnp.max(best, axis=1, keepdims=True)
        total = jnp.zeros((each, LANES), jnp.float32)
        found = jnp.zeros((each, LANES), jnp.float32)
        for v in values:
            total = total + v * jnp.exp(v[:, :1] - peak)
            found = found + v
        log_norm = peak + jnp.log(total[:, TOPK : TOPK + 1])
        token = found[:, TOPK + 1 : TOPK + 2] - log_norm
        left = jnp.full((each, 1), float(TOPK), jnp.float32)
        mass = jnp.zeros((each, 1), jnp.float32)
        top = peak
        for k in range(TOPK):
            hits = jnp.zeros((each, LANES), jnp.float32)
            for v in pool:
                hits = hits + jnp.where(v == top, 1.0, 0.0)
            count = jnp.minimum(jnp.sum(hits, axis=1, keepdims=True), left)
            mass = mass + jnp.where(count > 0.0, count * jnp.exp(top - log_norm), 0.0)
            left = left - count
            if k + 1 < TOPK:
                best = jnp.full((each, LANES), -jnp.inf, jnp.float32)
                for v in pool:
                    best = jnp.maximum(best, jnp.where(v < top, v, -jnp.inf))
                top = jnp.max(best, axis=1, keepdims=True)
        lp_ref[m : m + 1, :] = across(token)
        norm_ref[m : m + 1, :] = across(log_norm)
        mass_ref[m : m + 1, :] = across(mass)
        packs = [stats[m][s, each:] for s in range(sources)]
        highest = packs[0]
        for v in packs[1:]:
            highest = jnp.maximum(highest, v)
        total = jnp.zeros_like(highest)
        found = jnp.zeros_like(highest)
        for v in packs:
            total = total + v * pltpu.roll(jnp.exp(v - highest), groups, 0)
            found = found + v
        sums = jnp.zeros((SEQS, 1), jnp.float32)
        for g in range(groups):
            norm = highest[g : g + 1] + jnp.log(total[groups + g : groups + g + 1])
            token_row = found[2 * groups + g : 2 * groups + g + 1] - norm
            ids = jnp.broadcast_to(found[3 * groups + g : 3 * groups + g + 1], (SEQS, LANES))
            chosen = jnp.where(ids == seq_row, jnp.broadcast_to(token_row, (SEQS, LANES)), 0.0)
            sums = sums + jnp.sum(chosen, axis=1, keepdims=True)
        seq_out[m : m + 1, :] = jnp.sum(jnp.where(seq_lane == seq_place, sums, 0.0), axis=0, keepdims=True)


def finish(stats, each, groups):
    batches = len(stats)
    row = jax.ShapeDtypeStruct((batches, LANES), jnp.float32)
    lp, norm, mass, seq = pl.pallas_call(
        functools.partial(finish_kernel, batches=batches, each=each, groups=groups),
        out_shape=(row, row, row, row),
        name="finish",
    )(*stats)
    return lp[:, :each], norm[:, :each], mass[:, :each], seq[:, :SEQS]


def score(hidden_in, gain_ffn, w_gate, w_up, w_down, gain_final, head_weight, sampled_ids, seq_ids):
    batches, each, _ = hidden_in.shape
    size = lax.axis_size("vocab")
    devices = 2 * size
    section = lax.axis_index("section")
    place = lax.axis_index("vocab")
    owner = block_owner(size, section, place)
    first_column = (section * size + place) * head_weight.shape[1]
    ids = sampled_ids.reshape(batches, devices, each)[:, owner].reshape(batches, 1, devices * each) - first_column
    groups = devices * each // LANES
    own = jnp.arange(devices)[None, :, None] == section * size + place
    seq = jnp.where(own, seq_ids[:, None, :].astype(jnp.float32), 0.0).reshape(batches, groups, LANES)
    gathered = [gather_rows(rms_norm(hidden_in[m].astype(jnp.float32), gain_ffn), size) for m in range(batches)]
    stats = []
    for m in range(batches):
        parts = ffn(*gathered[m], w_gate, w_up, w_down)
        kept, came = scatter_sum(*parts, size)
        scaled = close_block(hidden_in, m, kept, came, gain_final)
        spread = gather_rows(scaled, size)
        part = head(owner, *spread, head_weight, ids[m], seq[m])
        stats.append(lax.all_to_all(part, AXES, split_axis=0, concat_axis=0, tiled=True))
    return finish(stats, each, groups)


def solution(mesh):
    in_specs = (
        P(None, AXES, None),
        P(),
        P(None, AXES),
        P(None, AXES),
        P(AXES, None),
        P(),
        P(None, AXES),
        P(),
        P(None, AXES),
    )
    out_specs = (P(None, AXES), P(None, AXES), P(None, AXES), P())
    return jax.shard_map(score, mesh=mesh, in_specs=in_specs, out_specs=out_specs, check_vma=False)
```

profile of v0, /device:TPU:0, one launch (start us, length us, event | category | flops | bytes accessed | tf_op | source)
XLA Modules:
  0.0 280.4 jit_solution(13535088836909427258)
XLA Ops:
  2.9 4.1 %collective-permute-start.15 = (bf16[8,7168]{1,0:T(8,128)(2,1)S(1)}, bf16[8,7168]{1,0:T(8,128)(2,1)S(1)}, u32[]{:S(2)}, u32[]{:S(2)}) collective-permute-start(bf16[8,7168]{1,0:T(8,128)(2,1)S(1)} %get-tuple-element.25), channel_id=1, source_target_pairs={{0,8},{1,9},{2,10},{3,11},{4,12},{5,13},{6,14},{7,15},{8,0},{9,1},... | collective-permute-start | bytes 344072 | tf_op jit(solution)/shard_map/ppermute | solution.py:70
  7.1 8.8 %collective-permute-done.15 = bf16[8,7168]{1,0:T(8,128)(2,1)S(1)} collective-permute-done((bf16[8,7168]{1,0:T(8,128)(2,1)S(1)}, bf16[8,7168]{1,0:T(8,128)(2,1)S(1)}, u32[]{:S(2)}, u32[]{:S(2)}) %collective-permute-start.15) | collective-permute-done | bytes 114720 | tf_op jit(solution)/shard_map/ppermute | solution.py:70
  18.4 6.1 %collective-permute-done.16 = bf16[16,7168]{1,0:T(8,128)(2,1)S(1)} collective-permute-done((bf16[16,7168]{1,0:T(8,128)(2,1)S(1)}, bf16[16,7168]{1,0:T(8,128)(2,1)S(1)}, u32[]{:S(2)}, u32[]{:S(2)}) %collective-permute-start.16) | collective-permute-done | bytes 229408 | tf_op jit(solution)/shard_map/ppermute | solution.py:70
  29.1 6.4 %collective-permute-done.17 = bf16[32,7168]{1,0:T(8,128)(2,1)S(1)} collective-permute-done((bf16[32,7168]{1,0:T(8,128)(2,1)S(1)}, bf16[32,7168]{1,0:T(8,128)(2,1)S(1)}, u32[]{:S(2)}, u32[]{:S(2)}) %collective-permute-start.17) | collective-permute-done | bytes 458784 | tf_op jit(solution)/shard_map/ppermute | solution.py:70
  35.6 2.4 collective-permute-start.18
  37.9 7.4 %collective-permute-done.2 = bf16[32,7168]{1,0:T(8,128)(2,1)S(1)} collective-permute-done((bf16[32,7168]{1,0:T(8,128)(2,1)S(1)}, bf16[32,7168]{1,0:T(8,128)(2,1)S(1)}, u32[]{:S(2)}, u32[]{:S(2)}) %collective-permute-start.2) | collective-permute-done | bytes 458784 | tf_op jit(solution)/shard_map/ppermute | solution.py:70
  45.4 2.4 collective-permute-start.3
  49.5 9.6 %collective-permute-done.3 = bf16[64,7168]{1,0:T(8,128)(2,1)S(1)} collective-permute-done((bf16[64,7168]{1,0:T(8,128)(2,1)S(1)}, bf16[64,7168]{1,0:T(8,128)(2,1)S(1)}, u32[]{:S(2)}, u32[]{:S(2)}) %collective-permute-start.3) | collective-permute-done | bytes 917536 | tf_op jit(solution)/shard_map/ppermute | solution.py:70
  59.3 15.3 %ffn.3 = (bf16[128,7168]{1,0:T(8,128)(2,1)S(1)}, bf16[128,7168]{1,0:T(8,128)(2,1)}) custom-call(bf16[128,7168]{1,0:T(8,128)(2,1)S(1)} %constant_dynamic-update-slice_fusion.10.near_ref, bf16[128,7168]{1,0:T(8,128)(2,1)S(1)} %collective-permute-done.19.far_ref, bf16[576,7168]{1,0:T(8,128)(2,1)} %bitcast.28, bf16[576,7168]{1,0:T(8,128)(2,1)} %bitcast.30, ...), custom_call_target="tpu_custom_call" | custom-call | flops 6341787648 | bytes 32112640 | tf_op jit(solution)/shard_map/ffn/pallas_call | solution.py:152
  75.1 15.4 %ffn.2 = (bf16[128,7168]{1,0:T(8,128)(2,1)S(1)}, bf16[128,7168]{1,0:T(8,128)(2,1)}) custom-call(bf16[128,7168]{1,0:T(8,128)(2,1)S(1)} %constant_dynamic-update-slice_fusion.near_ref, bf16[128,7168]{1,0:T(8,128)(2,1)S(1)} %collective-permute-done.4.far_ref, bf16[576,7168]{1,0:T(8,128)(2,1)} %bitcast.29, bf16[576,7168]{1,0:T(8,128)(2,1)} %bitcast.31, ...), custom_call_target="tpu_custom_call" | custom-call | flops 6341787648 | bytes 32112640 | tf_op jit(solution)/shard_map/ffn/pallas_call | solution.py:152
  91.0 2.5 add.82
  100.7 7.7 %collective-permute-done.21 = bf16[64,7168]{1,0:T(8,128)(2,1)} collective-permute-done((bf16[64,7168]{1,0:T(8,128)(2,1)S(1)}, bf16[64,7168]{1,0:T(8,128)(2,1)}, u32[]{:S(2)}, u32[]{:S(2)}) %collective-permute-start.21) | collective-permute-done | bytes 917536 | tf_op jit(solution)/shard_map/ppermute | solution.py:70
  109.7 2.1 collective-permute-start.22
  111.9 11.2 %collective-permute-done.6 = bf16[64,7168]{1,0:T(8,128)(2,1)S(1)} collective-permute-done((bf16[64,7168]{1,0:T(8,128)(2,1)S(1)}, bf16[64,7168]{1,0:T(8,128)(2,1)S(1)}, u32[]{:S(2)}, u32[]{:S(2)}) %collective-permute-start.6) | collective-permute-done | bytes 917536 | tf_op jit(solution)/shard_map/ppermute | solution.py:70
  125.5 6.3 %collective-permute-done.7 = bf16[32,7168]{1,0:T(8,128)(2,1)S(1)} collective-permute-done((bf16[32,7168]{1,0:T(8,128)(2,1)S(1)}, bf16[32,7168]{1,0:T(8,128)(2,1)S(1)}, u32[]{:S(2)}, u32[]{:S(2)}) %collective-permute-start.7) | collective-permute-done | bytes 458784 | tf_op jit(solution)/shard_map/ppermute | solution.py:70
  133.2 6.4 %collective-permute-done.8 = bf16[16,7168]{1,0:T(8,128)(2,1)S(1)} collective-permute-done((bf16[16,7168]{1,0:T(8,128)(2,1)S(1)}, bf16[16,7168]{1,0:T(8,128)(2,1)S(1)}, u32[]{:S(2)}, u32[]{:S(2)}) %collective-permute-start.8) | collective-permute-done | bytes 229408 | tf_op jit(solution)/shard_map/ppermute | solution.py:70
  140.0 3.0 %collective-permute-start.25 = (bf16[8,7168]{1,0:T(8,128)(2,1)S(1)}, bf16[8,7168]{1,0:T(8,128)(2,1)S(1)}, u32[]{:S(2)}, u32[]{:S(2)}) collective-permute-start(bf16[8,7168]{1,0:T(8,128)(2,1)S(1)} %close.3), channel_id=1, source_target_pairs={{0,8},{1,9},{2,10},{3,11},{4,12},{5,13},{6,14},{7,15},{8,0},{9,1},... | collective-permute-start | bytes 344072 | tf_op jit(solution)/shard_map/ppermute | solution.py:70
  143.0 6.4 %collective-permute-done.9.came_ref = bf16[8,7168]{1,0:T(8,128)(2,1)S(1)} collective-permute-done((bf16[8,7168]{1,0:T(8,128)(2,1)S(1)}, bf16[8,7168]{1,0:T(8,128)(2,1)S(1)}, u32[]{:S(2)}, u32[]{:S(2)}) %collective-permute-start.9) | collective-permute-done | bytes 114720 | tf_op jit(solution)/shard_map/ppermute | solution.py:70
  153.0 3.2 %collective-permute-done.10 = bf16[8,7168]{1,0:T(8,128)(2,1)S(1)} collective-permute-done((bf16[8,7168]{1,0:T(8,128)(2,1)S(1)}, bf16[8,7168]{1,0:T(8,128)(2,1)S(1)}, u32[]{:S(2)}, u32[]{:S(2)}) %collective-permute-start.10) | collective-permute-done | bytes 114720 | tf_op jit(solution)/shard_map/ppermute | solution.py:70
  157.0 3.2 %collective-permute-done.26 = bf16[16,7168]{1,0:T(8,128)(2,1)S(1)} collective-permute-done((bf16[16,7168]{1,0:T(8,128)(2,1)S(1)}, bf16[16,7168]{1,0:T(8,128)(2,1)S(1)}, u32[]{:S(2)}, u32[]{:S(2)}) %collective-permute-start.26) | collective-permute-done | bytes 229408 | tf_op jit(solution)/shard_map/ppermute | solution.py:70
  160.2 2.3 collective-permute-start.27
  162.7 2.3 collective-permute-start.12
  165.7 6.6 %collective-permute-done.27 = bf16[32,7168]{1,0:T(8,128)(2,1)S(1)} collective-permute-done((bf16[32,7168]{1,0:T(8,128)(2,1)S(1)}, bf16[32,7168]{1,0:T(8,128)(2,1)S(1)}, u32[]{:S(2)}, u32[]{:S(2)}) %collective-permute-start.27) | collective-permute-done | bytes 458784 | tf_op jit(solution)/shard_map/ppermute | solution.py:70
  172.4 2.3 collective-permute-start.28
  174.7 7.4 %collective-permute-done.12 = bf16[32,7168]{1,0:T(8,128)(2,1)S(1)} collective-permute-done((bf16[32,7168]{1,0:T(8,128)(2,1)S(1)}, bf16[32,7168]{1,0:T(8,128)(2,1)S(1)}, u32[]{:S(2)}, u32[]{:S(2)}) %collective-permute-start.12) | collective-permute-done | bytes 458784 | tf_op jit(solution)/shard_map/ppermute | solution.py:70
  182.2 2.3 collective-permute-start.13
  187.1 8.9 %collective-permute-done.13 = bf16[64,7168]{1,0:T(8,128)(2,1)S(1)} collective-permute-done((bf16[64,7168]{1,0:T(8,128)(2,1)S(1)}, bf16[64,7168]{1,0:T(8,128)(2,1)S(1)}, u32[]{:S(2)}, u32[]{:S(2)}) %collective-permute-start.13) | collective-permute-done | bytes 917536 | tf_op jit(solution)/shard_map/ppermute | solution.py:70
  197.3 29.2 %head.3 = f32[32,16,128]{2,1,0:T(8,128)} custom-call(s32[32]{0:T(128)S(1)} %pad_add_fusion.owner_ref, bf16[128,7168]{1,0:T(8,128)(2,1)S(1)} %constant_dynamic-update-slice_fusion.15.near_ref, bf16[128,7168]{1,0:T(8,128)(2,1)} %collective-permute-done.29.far_ref, bf16[4040,7168]{1,0:T(8,128)(2,1)} %bitcast.26, s32[1,256]{1,0:T(1,128)S(1)} %squeeze.16.ids_ref, ...), custom_call_target="tpu_custom_call" | custom-call | flops 14826864640 | bytes 61587456 | tf_op jit(solution)/shard_map/head/pallas_call | solution.py:321
  226.5 4.2 %all-to-all-start.1 = ((f32[32,16,128]{2,1,0:T(8,128)}), f32[32,16,128]{2,1,0:T(8,128)S(1)}, u32[]{:S(2)}, u32[]{:S(2)}) async-start(f32[32,16,128]{2,1,0:T(8,128)} %head.3), calls=%async_computation.1 | async-start | bytes 524288 | tf_op jit(solution)/shard_map/all_to_all | solution.py:445
  230.7 28.8 %head.2 = f32[32,16,128]{2,1,0:T(8,128)S(1)} custom-call(s32[32]{0:T(128)S(1)} %pad_add_fusion.owner_ref, bf16[128,7168]{1,0:T(8,128)(2,1)} %constant_dynamic-update-slice_fusion.5.near_ref, bf16[128,7168]{1,0:T(8,128)(2,1)} %collective-permute-done.14.far_ref, bf16[4040,7168]{1,0:T(8,128)(2,1)} %bitcast.27, s32[1,256]{1,0:T(1,128)S(1)} %squeeze.14.ids_ref, ...), custom_call_target="tpu_custom_call" | custom-call | flops 14826864640 | bytes 61587456 | tf_op jit(solution)/shard_map/head/pallas_call | solution.py:321
  259.5 16.9 %all_to_all.10.refs_0_ = f32[32,16,128]{2,1,0:T(8,128)} all-to-all(f32[32,16,128]{2,1,0:T(8,128)S(1)} %head.2), channel_id=1, replica_groups=mesh['section'=2,'vocab'=16] {'section','vocab'}, dimensions={0} | all-to-all | bytes 524288 | tf_op jit(solution)/shard_map/all_to_all | solution.py:445
  276.5 4.0 %finish.1 = (f32[2,128]{1,0:T(2,128)}, f32[2,128]{1,0:T(2,128)}, f32[2,128]{1,0:T(2,128)}, f32[2,128]{1,0:T(2,128)}) custom-call(f32[32,16,128]{2,1,0:T(8,128)} %all_to_all.10.refs_0_, f32[32,16,128]{2,1,0:T(8,128)} %copy-done.5), custom_call_target="tpu_custom_call" | custom-call | tf_op jit(solution)/shard_map/finish/pallas_call | solution.py:417
  (124 shorter events, 34.2 us)
Async XLA Ops:
  2.9 13.0 %collective-permute-start.15 = (bf16[8,7168]{1,0:T(8,128)(2,1)S(1)}, bf16[8,7168]{1,0:T(8,128)(2,1)S(1)}, u32[]{:S(2)}, u32[]{:S(2)}) collective-permute-start(bf16[8,7168]{1,0:T(8,128)(2,1)S(1)} %get-tuple-element.25), channel_id=1, source_target_pairs={{0,8},{1,9},{2,10},{3,11},{4,12},{5,13},{6,14},{7,15},{8,0},{9,1},... | collective-permute-start | bytes 344072 | tf_op jit(solution)/shard_map/ppermute | solution.py:70
  7.0 10.6 %collective-permute-start = (bf16[8,7168]{1,0:T(8,128)(2,1)S(1)}, bf16[8,7168]{1,0:T(8,128)(2,1)S(1)}, u32[]{:S(2)}, u32[]{:S(2)}) collective-permute-start(bf16[8,7168]{1,0:T(8,128)(2,1)S(1)} %get-tuple-element.29), channel_id=1, source_target_pairs={{0,8},{1,9},{2,10},{3,11},{4,12},{5,13},{6,14},{7,15},{8,0},{9,1},... | collective-permute-start | bytes 344072 | tf_op jit(solution)/shard_map/ppermute | solution.py:70
  16.0 8.5 %collective-permute-start.16 = (bf16[16,7168]{1,0:T(8,128)(2,1)S(1)}, bf16[16,7168]{1,0:T(8,128)(2,1)S(1)}, u32[]{:S(2)}, u32[]{:S(2)}) collective-permute-start(bf16[16,7168]{1,0:T(8,128)(2,1)S(1)} %pad_maximum_fusion.10), channel_id=1, source_target_pairs={{0,4},{1,5},{2,6},{3,7},{4,0},{5,1},{6,2},{7,3},{8,12},{9,13},{10,... | collective-permute-start | bytes 688136 | tf_op jit(solution)/shard_map/ppermute | solution.py:70
  17.6 9.8 %collective-permute-start.1 = (bf16[16,7168]{1,0:T(8,128)(2,1)S(1)}, bf16[16,7168]{1,0:T(8,128)(2,1)S(1)}, u32[]{:S(2)}, u32[]{:S(2)}) collective-permute-start(bf16[16,7168]{1,0:T(8,128)(2,1)S(1)} %pad_maximum_fusion.8), channel_id=1, source_target_pairs={{0,4},{1,5},{2,6},{3,7},{4,0},{5,1},{6,2},{7,3},{8,12},{9,13},{10,... | collective-permute-start | bytes 688136 | tf_op jit(solution)/shard_map/ppermute | solution.py:70
  24.5 10.9 %collective-permute-start.17 = (bf16[32,7168]{1,0:T(8,128)(2,1)S(1)}, bf16[32,7168]{1,0:T(8,128)(2,1)S(1)}, u32[]{:S(2)}, u32[]{:S(2)}) collective-permute-start(bf16[32,7168]{1,0:T(8,128)(2,1)S(1)} %pad_maximum_fusion.6), channel_id=1, source_target_pairs={{0,2},{1,3},{2,0},{3,1},{4,6},{5,7},{6,4},{7,5},{8,10},{9,11},{10,... | collective-permute-start | bytes 1376264 | tf_op jit(solution)/shard_map/ppermute | solution.py:70
  27.4 17.9 %collective-permute-start.2 = (bf16[32,7168]{1,0:T(8,128)(2,1)S(1)}, bf16[32,7168]{1,0:T(8,128)(2,1)S(1)}, u32[]{:S(2)}, u32[]{:S(2)}) collective-permute-start(bf16[32,7168]{1,0:T(8,128)(2,1)S(1)} %pad_maximum_fusion.4), channel_id=1, source_target_pairs={{0,2},{1,3},{2,0},{3,1},{4,6},{5,7},{6,4},{7,5},{8,10},{9,11},{10,... | collective-permute-start | bytes 1376264 | tf_op jit(solution)/shard_map/ppermute | solution.py:70
  35.6 13.8 %collective-permute-start.18 = (bf16[64,7168]{1,0:T(8,128)(2,1)S(1)}, bf16[64,7168]{1,0:T(8,128)(2,1)S(1)}, u32[]{:S(2)}, u32[]{:S(2)}) collective-permute-start(bf16[64,7168]{1,0:T(8,128)(2,1)S(1)} %pad_maximum_fusion.2), channel_id=1, source_target_pairs={{0,1},{1,0},{2,3},{3,2},{4,5},{5,4},{6,7},{7,6},{8,9},{9,8},{10,11... | collective-permute-start | bytes 2752520 | tf_op jit(solution)/shard_map/ppermute | solution.py:70
  45.4 13.8 %collective-permute-start.3 = (bf16[64,7168]{1,0:T(8,128)(2,1)S(1)}, bf16[64,7168]{1,0:T(8,128)(2,1)S(1)}, u32[]{:S(2)}, u32[]{:S(2)}) collective-permute-start(bf16[64,7168]{1,0:T(8,128)(2,1)S(1)} %pad_maximum_fusion), channel_id=1, source_target_pairs={{0,1},{1,0},{2,3},{3,2},{4,5},{5,4},{6,7},{7,6},{8,9},{9,8},{10,11... | collective-permute-start | bytes 2752520 | tf_op jit(solution)/shard_map/ppermute | solution.py:70
  49.4 9.9 %collective-permute-start.19 = (bf16[128,7168]{1,0:T(8,128)(2,1)S(1)}, bf16[128,7168]{1,0:T(8,128)(2,1)S(1)}, u32[]{:S(2)}, u32[]{:S(2)}) collective-permute-start(bf16[128,7168]{1,0:T(8,128)(2,1)S(1)} %constant_dynamic-update-slice_fusion.10.near_ref), channel_id=1, source_target_pairs={{0,16},{1,17},{2,18},{3,19},{4,20},{5,21},{6,22},{7,23},{8,24},{9,... | collective-permute-start | bytes 5505032 | tf_op jit(solution)/shard_map/ppermute | solution.py:70
  59.2 15.9 %collective-permute-start.4 = (bf16[128,7168]{1,0:T(8,128)(2,1)S(1)}, bf16[128,7168]{1,0:T(8,128)(2,1)S(1)}, u32[]{:S(2)}, u32[]{:S(2)}) collective-permute-start(bf16[128,7168]{1,0:T(8,128)(2,1)S(1)} %constant_dynamic-update-slice_fusion.near_ref), channel_id=1, source_target_pairs={{0,16},{1,17},{2,18},{3,19},{4,20},{5,21},{6,22},{7,23},{8,24},{9,... | collective-permute-start | bytes 5505032 | tf_op jit(solution)/shard_map/ppermute | solution.py:70
  74.6 16.4 %collective-permute-start.20 = (bf16[128,7168]{1,0:T(8,128)(2,1)}, bf16[128,7168]{1,0:T(8,128)(2,1)}, u32[]{:S(2)}, u32[]{:S(2)}) collective-permute-start(bf16[128,7168]{1,0:T(8,128)(2,1)} %get-tuple-element.15), channel_id=1, source_target_pairs={{0,16},{1,17},{2,18},{3,19},{4,20},{5,21},{6,22},{7,23},{8,24},{9,... | collective-permute-start | bytes 5505032 | tf_op jit(solution)/shard_map/ppermute | solution.py:70
  90.5 7.6 %collective-permute-start.5 = (bf16[128,7168]{1,0:T(8,128)(2,1)}, bf16[128,7168]{1,0:T(8,128)(2,1)}, u32[]{:S(2)}, u32[]{:S(2)}) collective-permute-start(bf16[128,7168]{1,0:T(8,128)(2,1)} %get-tuple-element.13), channel_id=1, source_target_pairs={{0,16},{1,17},{2,18},{3,19},{4,20},{5,21},{6,22},{7,23},{8,24},{9,... | collective-permute-start | bytes 5505032 | tf_op jit(solution)/shard_map/ppermute | solution.py:70
  94.8 13.6 %collective-permute-start.21 = (bf16[64,7168]{1,0:T(8,128)(2,1)S(1)}, bf16[64,7168]{1,0:T(8,128)(2,1)}, u32[]{:S(2)}, u32[]{:S(2)}) collective-permute-start(bf16[64,7168]{1,0:T(8,128)(2,1)S(1)} %slice.121), channel_id=1, source_target_pairs={{0,1},{1,0},{2,3},{3,2},{4,5},{5,4},{6,7},{7,6},{8,9},{9,8},{10,11... | collective-permute-start | bytes 2752520 | tf_op jit(solution)/shard_map/ppermute | solution.py:70
  100.1 22.9 %collective-permute-start.6 = (bf16[64,7168]{1,0:T(8,128)(2,1)S(1)}, bf16[64,7168]{1,0:T(8,128)(2,1)S(1)}, u32[]{:S(2)}, u32[]{:S(2)}) collective-permute-start(bf16[64,7168]{1,0:T(8,128)(2,1)S(1)} %slice.111), channel_id=1, source_target_pairs={{0,1},{1,0},{2,3},{3,2},{4,5},{5,4},{6,7},{7,6},{8,9},{9,8},{10,11... | collective-permute-start | bytes 2752520 | tf_op jit(solution)/shard_map/ppermute | solution.py:70
  109.7 15.6 %collective-permute-start.22 = (bf16[32,7168]{1,0:T(8,128)(2,1)S(1)}, bf16[32,7168]{1,0:T(8,128)(2,1)S(1)}, u32[]{:S(2)}, u32[]{:S(2)}) collective-permute-start(bf16[32,7168]{1,0:T(8,128)(2,1)S(1)} %slice.123), channel_id=1, source_target_pairs={{0,2},{1,3},{2,0},{3,1},{4,6},{5,7},{6,4},{7,5},{8,10},{9,11},{10,... | collective-permute-start | bytes 1376264 | tf_op jit(solution)/shard_map/ppermute | solution.py:70
  123.2 8.6 %collective-permute-start.7 = (bf16[32,7168]{1,0:T(8,128)(2,1)S(1)}, bf16[32,7168]{1,0:T(8,128)(2,1)S(1)}, u32[]{:S(2)}, u32[]{:S(2)}) collective-permute-start(bf16[32,7168]{1,0:T(8,128)(2,1)S(1)} %slice.113), channel_id=1, source_target_pairs={{0,2},{1,3},{2,0},{3,1},{4,6},{5,7},{6,4},{7,5},{8,10},{9,11},{10,... | collective-permute-start | bytes 1376264 | tf_op jit(solution)/shard_map/ppermute | solution.py:70
  125.4 6.5 %collective-permute-start.23 = (bf16[16,7168]{1,0:T(8,128)(2,1)S(1)}, bf16[16,7168]{1,0:T(8,128)(2,1)S(1)}, u32[]{:S(2)}, u32[]{:S(2)}) collective-permute-start(bf16[16,7168]{1,0:T(8,128)(2,1)S(1)} %slice.125), channel_id=1, source_target_pairs={{0,4},{1,5},{2,6},{3,7},{4,0},{5,1},{6,2},{7,3},{8,12},{9,13},{10,... | collective-permute-start | bytes 688136 | tf_op jit(solution)/shard_map/ppermute | solution.py:70
  131.8 7.8 %collective-permute-start.8 = (bf16[16,7168]{1,0:T(8,128)(2,1)S(1)}, bf16[16,7168]{1,0:T(8,128)(2,1)S(1)}, u32[]{:S(2)}, u32[]{:S(2)}) collective-permute-start(bf16[16,7168]{1,0:T(8,128)(2,1)S(1)} %slice.115), channel_id=1, source_target_pairs={{0,4},{1,5},{2,6},{3,7},{4,0},{5,1},{6,2},{7,3},{8,12},{9,13},{10,... | collective-permute-start | bytes 688136 | tf_op jit(solution)/shard_map/ppermute | solution.py:70
  132.0 7.8 %collective-permute-start.24 = (bf16[8,7168]{1,0:T(8,128)(2,1)S(1)}, bf16[8,7168]{1,0:T(8,128)(2,1)S(1)}, u32[]{:S(2)}, u32[]{:S(2)}) collective-permute-start(bf16[8,7168]{1,0:T(8,128)(2,1)S(1)} %get-tuple-element.30), channel_id=1, source_target_pairs={{0,8},{1,9},{2,10},{3,11},{4,12},{5,13},{6,14},{7,15},{8,0},{9,1},... | collective-permute-start | bytes 344072 | tf_op jit(solution)/shard_map/ppermute | solution.py:70
  139.7 9.6 %collective-permute-start.9 = (bf16[8,7168]{1,0:T(8,128)(2,1)S(1)}, bf16[8,7168]{1,0:T(8,128)(2,1)S(1)}, u32[]{:S(2)}, u32[]{:S(2)}) collective-permute-start(bf16[8,7168]{1,0:T(8,128)(2,1)S(1)} %get-tuple-element.32), channel_id=1, source_target_pairs={{0,8},{1,9},{2,10},{3,11},{4,12},{5,13},{6,14},{7,15},{8,0},{9,1},... | collective-permute-start | bytes 344072 | tf_op jit(solution)/shard_map/ppermute | solution.py:70
  140.0 11.6 %collective-permute-start.25 = (bf16[8,7168]{1,0:T(8,128)(2,1)S(1)}, bf16[8,7168]{1,0:T(8,128)(2,1)S(1)}, u32[]{:S(2)}, u32[]{:S(2)}) collective-permute-start(bf16[8,7168]{1,0:T(8,128)(2,1)S(1)} %close.3), channel_id=1, source_target_pairs={{0,8},{1,9},{2,10},{3,11},{4,12},{5,13},{6,14},{7,15},{8,0},{9,1},... | collective-permute-start | bytes 344072 | tf_op jit(solution)/shard_map/ppermute | solution.py:70
  149.5 6.7 %collective-permute-start.10 = (bf16[8,7168]{1,0:T(8,128)(2,1)S(1)}, bf16[8,7168]{1,0:T(8,128)(2,1)S(1)}, u32[]{:S(2)}, u32[]{:S(2)}) collective-permute-start(bf16[8,7168]{1,0:T(8,128)(2,1)S(1)} %close.2), channel_id=1, source_target_pairs={{0,8},{1,9},{2,10},{3,11},{4,12},{5,13},{6,14},{7,15},{8,0},{9,1},... | collective-permute-start | bytes 344072 | tf_op jit(solution)/shard_map/ppermute | solution.py:70
  151.6 8.5 %collective-permute-start.26 = (bf16[16,7168]{1,0:T(8,128)(2,1)S(1)}, bf16[16,7168]{1,0:T(8,128)(2,1)S(1)}, u32[]{:S(2)}, u32[]{:S(2)}) collective-permute-start(bf16[16,7168]{1,0:T(8,128)(2,1)S(1)} %pad_maximum_fusion.11), channel_id=1, source_target_pairs={{0,4},{1,5},{2,6},{3,7},{4,0},{5,1},{6,2},{7,3},{8,12},{9,13},{10,... | collective-permute-start | bytes 688136 | tf_op jit(solution)/shard_map/ppermute | solution.py:70
  156.2 6.4 %collective-permute-start.11 = (bf16[16,7168]{1,0:T(8,128)(2,1)S(1)}, bf16[16,7168]{1,0:T(8,128)(2,1)S(1)}, u32[]{:S(2)}, u32[]{:S(2)}) collective-permute-start(bf16[16,7168]{1,0:T(8,128)(2,1)S(1)} %pad_maximum_fusion.9), channel_id=1, source_target_pairs={{0,4},{1,5},{2,6},{3,7},{4,0},{5,1},{6,2},{7,3},{8,12},{9,13},{10,... | collective-permute-start | bytes 688136 | tf_op jit(solution)/shard_map/ppermute | solution.py:70
  160.2 12.1 %collective-permute-start.27 = (bf16[32,7168]{1,0:T(8,128)(2,1)S(1)}, bf16[32,7168]{1,0:T(8,128)(2,1)S(1)}, u32[]{:S(2)}, u32[]{:S(2)}) collective-permute-start(bf16[32,7168]{1,0:T(8,128)(2,1)S(1)} %pad_maximum_fusion.7), channel_id=1, source_target_pairs={{0,2},{1,3},{2,0},{3,1},{4,6},{5,7},{6,4},{7,5},{8,10},{9,11},{10,... | collective-permute-start | bytes 1376264 | tf_op jit(solution)/shard_map/ppermute | solution.py:70
  162.7 19.5 %collective-permute-start.12 = (bf16[32,7168]{1,0:T(8,128)(2,1)S(1)}, bf16[32,7168]{1,0:T(8,128)(2,1)S(1)}, u32[]{:S(2)}, u32[]{:S(2)}) collective-permute-start(bf16[32,7168]{1,0:T(8,128)(2,1)S(1)} %pad_maximum_fusion.5), channel_id=1, source_target_pairs={{0,2},{1,3},{2,0},{3,1},{4,6},{5,7},{6,4},{7,5},{8,10},{9,11},{10,... | collective-permute-start | bytes 1376264 | tf_op jit(solution)/shard_map/ppermute | solution.py:70
  172.4 13.7 %collective-permute-start.28 = (bf16[64,7168]{1,0:T(8,128)(2,1)S(1)}, bf16[64,7168]{1,0:T(8,128)(2,1)S(1)}, u32[]{:S(2)}, u32[]{:S(2)}) collective-permute-start(bf16[64,7168]{1,0:T(8,128)(2,1)S(1)} %pad_maximum_fusion.3), channel_id=1, source_target_pairs={{0,1},{1,0},{2,3},{3,2},{4,5},{5,4},{6,7},{7,6},{8,9},{9,8},{10,11... | collective-permute-start | bytes 2752520 | tf_op jit(solution)/shard_map/ppermute | solution.py:70
  182.2 13.7 %collective-permute-start.13 = (bf16[64,7168]{1,0:T(8,128)(2,1)S(1)}, bf16[64,7168]{1,0:T(8,128)(2,1)S(1)}, u32[]{:S(2)}, u32[]{:S(2)}) collective-permute-start(bf16[64,7168]{1,0:T(8,128)(2,1)S(1)} %pad_maximum_fusion.1), channel_id=1, source_target_pairs={{0,1},{1,0},{2,3},{3,2},{4,5},{5,4},{6,7},{7,6},{8,9},{9,8},{10,11... | collective-permute-start | bytes 2752520 | tf_op jit(solution)/shard_map/ppermute | solution.py:70
  186.2 11.2 %collective-permute-start.29 = (bf16[128,7168]{1,0:T(8,128)(2,1)S(1)}, bf16[128,7168]{1,0:T(8,128)(2,1)}, u32[]{:S(2)}, u32[]{:S(2)}) collective-permute-start(bf16[128,7168]{1,0:T(8,128)(2,1)S(1)} %constant_dynamic-update-slice_fusion.15.near_ref), channel_id=1, source_target_pairs={{0,16},{1,17},{2,18},{3,19},{4,20},{5,21},{6,22},{7,23},{8,24},{9,... | collective-permute-start | bytes 5505032 | tf_op jit(solution)/shard_map/ppermute | solution.py:70
  197.0 33.7 %collective-permute-start.14 = (bf16[128,7168]{1,0:T(8,128)(2,1)}, bf16[128,7168]{1,0:T(8,128)(2,1)}, u32[]{:S(2)}, u32[]{:S(2)}) collective-permute-start(bf16[128,7168]{1,0:T(8,128)(2,1)} %constant_dynamic-update-slice_fusion.5.near_ref), channel_id=1, source_target_pairs={{0,16},{1,17},{2,18},{3,19},{4,20},{5,21},{6,22},{7,23},{8,24},{9,... | collective-permute-start | bytes 5505032 | tf_op jit(solution)/shard_map/ppermute | solution.py:70
  226.5 33.0 %all-to-all-start.1 = ((f32[32,16,128]{2,1,0:T(8,128)}), f32[32,16,128]{2,1,0:T(8,128)S(1)}, u32[]{:S(2)}, u32[]{:S(2)}) async-start(f32[32,16,128]{2,1,0:T(8,128)} %head.3), calls=%async_computation.1 | async-start | bytes 524288 | tf_op jit(solution)/shard_map/all_to_all | solution.py:445
  259.5 16.9 %copy-start.5 = (f32[32,16,128]{2,1,0:T(8,128)}, f32[32,16,128]{2,1,0:T(8,128)S(1)}, u32[]{:S(2)}) copy-start(f32[32,16,128]{2,1,0:T(8,128)S(1)} %all-to-all-done.1.refs_1_) | copy-start | bytes 786436
  (9 other events, 64.0 us)
where the time goes:
time: 281 us; the launch traced here: 280 us
  waiting for transfers between devices  113 us (40%)
  Pallas kernels  93 us (33%)
  starting transfers between devices  40.8 us (15%)
  blocking collectives  16.9 us (6%)
  other arithmetic  9 us (3%)
  local copies, waits for them, and re-layouts  6.91 us (2%)
    ppermute x30, waiting for transfers between devices, move(): return lax.ppermute(rows, AXES, perm)  113 us
    pallas_call x2, Pallas kernels, head(): pl.pallas_call(functools.partial(head_kernel, steps=steps, width=width, e...  58 us
    ppermute x30, starting transfers between devices, move(): return lax.ppermute(rows, AXES, perm)  36.7 us
    pallas_call x2, Pallas kernels, ffn(): pl.pallas_call(functools.partial(ffn_kernel, steps=steps), grid=(steps +...  30.7 us
    all_to_all x1, blocking collectives, score(): lax.all_to_all(part, AXES, split_axis=0, concat_axis=0, tiled=True)  16.9 us
  transfers between devices with their start and end apart: 31, of which 21 were waited for; matrix products, arithmetic and copies ran while one was open for 4% of the time, Pallas kernels for 32%

commit v1 on v0

--- a/solution.py
+++ b/solution.py
@@ -14,6 +14,7 @@
 NET = 32
 FFN_VMEM = 40 << 20
 HEAD_VMEM = 40 << 20
+HEAD_TILE = 680
 AXES = ("section", "vocab")
 epsilon = 1e-06
 
@@ -214,10 +215,41 @@
     return c[:TOPK]
 
 
-def head_kernel(
-    owner_ref, near_ref, far_ref, w_ref, ids_ref, seq_ref, out_ref, x_ref, logits_ref, stat_ref, table_ref, pack_ref,
-    *, steps, width, each
-):
+def early_kernel(near_ref, far_ref, w_ref, out_ref, x_ref):
+    half = near_ref.shape[0]
+
+    @pl.when(pl.program_id(0) == 0)
+    def _():
+        x_ref[:half] = near_ref[...]
+        x_ref[half:] = far_ref[...]
+
+    out_ref[...] = turned_dot(w_ref[...], x_ref[...])
+
+
+def early_head(near, far, w, steps, tile=HEAD_TILE):
+    half, depth = near.shape
+    rows = 2 * half
+    return pl.pallas_call(
+        early_kernel,
+        grid=(steps,),
+        in_specs=[
+            pl.BlockSpec((half, depth), lambda i: (0, 0), pipeline_mode=pl.Buffered(1)),
+            pl.BlockSpec((half, depth), lambda i: (0, 0), pipeline_mode=pl.Buffered(1)),
+            pl.BlockSpec((tile, depth), lambda i: (i, 0)),
+        ],
+        out_specs=pl.BlockSpec((tile, rows), lambda i: (i, 0)),
+        out_shape=jax.ShapeDtypeStruct((steps * tile, rows), jnp.float32),
+        scratch_shapes=[pltpu.VMEM((rows, depth), jnp.bfloat16)],
+        cost_estimate=pl.CostEstimate(
+            flops=2 * rows * depth * steps * tile, bytes_accessed=2 * depth * (steps * tile + rows), transcendentals=0
+        ),
+        compiler_params=pltpu.CompilerParams(vmem_limit_bytes=HEAD_VMEM),
+        name="early_head",
+    )(near, far, w.T)
+
+
+def head_kernel(owner_ref, near_ref, far_ref, w_ref, ids_ref, seq_ref, *refs, steps, width, each, skip):
+    early_refs, (out_ref, x_ref, logits_ref, stat_ref, table_ref, pack_ref) = refs[:-6], refs[-6:]
     i = pl.program_id(0)
     half = near_ref.shape[0]
     tile = w_ref.shape[0]
@@ -226,8 +258,10 @@
     def _():
         x_ref[:half] = near_ref[...]
         x_ref[half:] = far_ref[...]
-
-    logits_ref[pl.ds(pl.multiple_of(i * tile, tile), tile), :] = turned_dot(w_ref[...], x_ref[...])
+        for early_ref in early_refs:
+            logits_ref[: early_ref.shape[0]] = early_ref[...]
+
+    logits_ref[pl.ds(pl.multiple_of((i + skip) * tile, tile), tile), :] = turned_dot(w_ref[...], x_ref[...])
 
     @pl.when(i == steps - 1)
     def _():
@@ -309,7 +343,7 @@
         out_ref[:, each:, :] = jnp.broadcast_to(pack_ref[...][None], (out_ref.shape[0],) + pack_ref.shape)
 
 
-def head(owner, near, far, w, ids, seq, tile=680):
+def head(owner, near, far, w, ids, seq, early=(), tile=HEAD_TILE):
     half, depth = near.shape
     rows = 2 * half
     width = w.shape[1]
@@ -317,23 +351,25 @@
     each = rows // devices
     groups = rows // LANES
     packed = -(-4 * groups // 8) * 8
-    steps = -(-width // tile)
+    skip = sum(e.shape[0] for e in early) // tile
+    steps = -(-width // tile) - skip
     return pl.pallas_call(
-        functools.partial(head_kernel, steps=steps, width=width, each=each),
+        functools.partial(head_kernel, steps=steps, width=width, each=each, skip=skip),
         grid_spec=pltpu.PrefetchScalarGridSpec(
             num_scalar_prefetch=1,
             grid=(steps,),
             in_specs=[
                 pl.BlockSpec((half, depth), lambda i, o: (0, 0), pipeline_mode=pl.Buffered(1)),
                 pl.BlockSpec((half, depth), lambda i, o: (0, 0), pipeline_mode=pl.Buffered(1)),
-                pl.BlockSpec((tile, depth), lambda i, o: (i, 0)),
+                pl.BlockSpec((tile, depth), lambda i, o: (i + skip, 0)),
                 pl.BlockSpec((1, rows), lambda i, o: (0, 0)),
                 pl.BlockSpec((groups, LANES), lambda i, o: (0, 0)),
-            ],
+            ]
+            + [pl.BlockSpec(e.shape, lambda i, o: (0, 0), pipeline_mode=pl.Buffered(1)) for e in early],
             out_specs=pl.BlockSpec((devices, each + packed, LANES), lambda i, o: (0, 0, 0)),
             scratch_shapes=[
                 pltpu.VMEM((rows, depth), jnp.bfloat16),
-                pltpu.VMEM((steps * tile, rows), jnp.float32),
+                pltpu.VMEM(((steps + skip) * tile, rows), jnp.float32),
                 pltpu.VMEM((LANES, LANES), jnp.float32),
                 pltpu.VMEM((rows, LANES), jnp.float32),
                 pltpu.VMEM((packed, LANES), jnp.float32),
@@ -341,11 +377,13 @@
         ),
         out_shape=jax.ShapeDtypeStruct((devices, each + packed, LANES), jnp.float32),
         cost_estimate=pl.CostEstimate(
-            flops=2 * rows * depth * width, bytes_accessed=2 * depth * (width + rows), transcendentals=rows * width
+            flops=2 * rows * depth * (width - skip * tile),
+            bytes_accessed=2 * depth * (width - skip * tile + rows),
+            transcendentals=rows * width,
         ),
         compiler_params=pltpu.CompilerParams(vmem_limit_bytes=HEAD_VMEM),
         name="head",
-    )(owner, near, far, w.T, ids, seq)
+    )(owner, near, far, w.T, ids, seq, *early)
 
 
 def finish_kernel(*refs, batches, each, groups):
@@ -441,7 +479,11 @@
         kept, came = scatter_sum(*parts, size)
         scaled = close_block(hidden_in, m, kept, came, gain_final)
         spread = gather_rows(scaled, size)
-        part = head(owner, *spread, head_weight, ids[m], seq[m])
+        early = ()
+        steps = -(-head_weight.shape[1] // HEAD_TILE)
+        if m + 1 < batches and steps > 1:
+            early = (early_head(*spread, head_weight, steps // 2),)
+        part = head(owner, *spread, head_weight, ids[m], seq[m], early)
         stats.append(lax.all_to_all(part, AXES, split_axis=0, concat_axis=0, tiled=True))
     return finish(stats, each, groups)
 

time: 281 us -> 284 us (1.011)
  Pallas kernels: 93 us -> 97.2 us
    pallas_call x0 -> x1, Pallas kernels: none -> 13.8 us  [early_head(): pl.pallas_call(early_kernel, grid=(steps,), in_specs=[pl.BlockSpec((half,...]
    pallas_call x2, Pallas kernels: 58 us -> 48.3 us  [head(): pl.pallas_call(functools.partial(head_kernel, steps=steps, width=width, e...]
  transfers between devices with their start and end apart: 31 -> 31, of which waited for: 21 -> 21; matrix products, arithmetic and copies ran while one was open for 4% -> 4% of each run, Pallas kernels for 32% -> 33%
where the time goes in v1:
time: 284 us
  waiting for transfers between devices  112 us (39%)
  Pallas kernels  97.2 us (34%)
  starting transfers between devices  40.2 us (14%)
  blocking collectives  16.9 us (6%)
  other arithmetic  9.01 us (3%)
  local copies, waits for them, and re-layouts  6.91 us (2%)
    ppermute x30, waiting for transfers between devices, move(): return lax.ppermute(rows, AXES, perm)  112 us
    pallas_call x2, Pallas kernels, head(): pl.pallas_call(functools.partial(head_kernel, steps=steps, width=width, e...  48.3 us
    ppermute x30, starting transfers between devices, move(): return lax.ppermute(rows, AXES, perm)  36.1 us
    pallas_call x2, Pallas kernels, ffn(): pl.pallas_call(functools.partial(ffn_kernel, steps=steps), grid=(steps +...  30.7 us
    all_to_all x1, blocking collectives, score(): lax.all_to_all(part, AXES, split_axis=0, concat_axis=0, tiled=True)  16.9 us
    pallas_call x1, Pallas kernels, early_head(): pl.pallas_call(early_kernel, grid=(steps,), in_specs=[pl.BlockSpec((half,...  13.8 us
  transfers between devices with their start and end apart: 31, of which 21 were waited for; matrix products, arithmetic and copies ran while one was open for 4% of the time, Pallas kernels for 33%

profile of v1, /device:TPU:0, one launch (start us, length us, event | category | flops | bytes accessed | tf_op | source)
XLA Modules:
  0.0 283.8 jit_solution(3156179956301350413)
XLA Ops:
  2.9 4.1 %collective-permute-start.15 = (bf16[8,7168]{1,0:T(8,128)(2,1)S(1)}, bf16[8,7168]{1,0:T(8,128)(2,1)S(1)}, u32[]{:S(2)}, u32[]{:S(2)}) collective-permute-start(bf16[8,7168]{1,0:T(8,128)(2,1)S(1)} %get-tuple-element.25), channel_id=1, source_target_pairs={{0,8},{1,9},{2,10},{3,11},{4,12},{5,13},{6,14},{7,15},{8,0},{9,1},... | collective-permute-start | bytes 344072 | tf_op jit(solution)/shard_map/ppermute | solution.py:71
  7.1 8.8 %collective-permute-done.15 = bf16[8,7168]{1,0:T(8,128)(2,1)S(1)} collective-permute-done((bf16[8,7168]{1,0:T(8,128)(2,1)S(1)}, bf16[8,7168]{1,0:T(8,128)(2,1)S(1)}, u32[]{:S(2)}, u32[]{:S(2)}) %collective-permute-start.15) | collective-permute-done | bytes 114720 | tf_op jit(solution)/shard_map/ppermute | solution.py:71
  18.4 6.1 %collective-permute-done.16 = bf16[16,7168]{1,0:T(8,128)(2,1)S(1)} collective-permute-done((bf16[16,7168]{1,0:T(8,128)(2,1)S(1)}, bf16[16,7168]{1,0:T(8,128)(2,1)S(1)}, u32[]{:S(2)}, u32[]{:S(2)}) %collective-permute-start.16) | collective-permute-done | bytes 229408 | tf_op jit(solution)/shard_map/ppermute | solution.py:71
  29.1 6.4 %collective-permute-done.17 = bf16[32,7168]{1,0:T(8,128)(2,1)S(1)} collective-permute-done((bf16[32,7168]{1,0:T(8,128)(2,1)S(1)}, bf16[32,7168]{1,0:T(8,128)(2,1)S(1)}, u32[]{:S(2)}, u32[]{:S(2)}) %collective-permute-start.17) | collective-permute-done | bytes 458784 | tf_op jit(solution)/shard_map/ppermute | solution.py:71
  35.6 2.4 collective-permute-start.18
  37.9 7.4 %collective-permute-done.2 = bf16[32,7168]{1,0:T(8,128)(2,1)S(1)} collective-permute-done((bf16[32,7168]{1,0:T(8,128)(2,1)S(1)}, bf16[32,7168]{1,0:T(8,128)(2,1)S(1)}, u32[]{:S(2)}, u32[]{:S(2)}) %collective-permute-start.2) | collective-permute-done | bytes 458784 | tf_op jit(solution)/shard_map/ppermute | solution.py:71
  45.4 2.4 collective-permute-start.3
  49.5 9.6 %collective-permute-done.3 = bf16[64,7168]{1,0:T(8,128)(2,1)S(1)} collective-permute-done((bf16[64,7168]{1,0:T(8,128)(2,1)S(1)}, bf16[64,7168]{1,0:T(8,128)(2,1)S(1)}, u32[]{:S(2)}, u32[]{:S(2)}) %collective-permute-start.3) | collective-permute-done | bytes 917536 | tf_op jit(solution)/shard_map/ppermute | solution.py:71
  59.3 15.3 %ffn.3 = (bf16[128,7168]{1,0:T(8,128)(2,1)S(1)}, bf16[128,7168]{1,0:T(8,128)(2,1)}) custom-call(bf16[128,7168]{1,0:T(8,128)(2,1)S(1)} %constant_dynamic-update-slice_fusion.10.near_ref, bf16[128,7168]{1,0:T(8,128)(2,1)S(1)} %collective-permute-done.19.far_ref, bf16[576,7168]{1,0:T(8,128)(2,1)} %bitcast.29, bf16[576,7168]{1,0:T(8,128)(2,1)} %bitcast.31, ...), custom_call_target="tpu_custom_call" | custom-call | flops 6341787648 | bytes 32112640 | tf_op jit(solution)/shard_map/ffn/pallas_call | solution.py:153
  75.1 15.4 %ffn.2 = (bf16[128,7168]{1,0:T(8,128)(2,1)S(1)}, bf16[128,7168]{1,0:T(8,128)(2,1)}) custom-call(bf16[128,7168]{1,0:T(8,128)(2,1)S(1)} %constant_dynamic-update-slice_fusion.near_ref, bf16[128,7168]{1,0:T(8,128)(2,1)S(1)} %collective-permute-done.4.far_ref, bf16[576,7168]{1,0:T(8,128)(2,1)} %bitcast.30, bf16[576,7168]{1,0:T(8,128)(2,1)} %bitcast.32, ...), custom_call_target="tpu_custom_call" | custom-call | flops 6341787648 | bytes 32112640 | tf_op jit(solution)/shard_map/ffn/pallas_call | solution.py:153
  91.0 2.5 add.82
  100.7 7.7 %collective-permute-done.21 = bf16[64,7168]{1,0:T(8,128)(2,1)} collective-permute-done((bf16[64,7168]{1,0:T(8,128)(2,1)S(1)}, bf16[64,7168]{1,0:T(8,128)(2,1)}, u32[]{:S(2)}, u32[]{:S(2)}) %collective-permute-start.21) | collective-permute-done | bytes 917536 | tf_op jit(solution)/shard_map/ppermute | solution.py:71
  111.9 11.2 %collective-permute-done.6 = bf16[64,7168]{1,0:T(8,128)(2,1)S(1)} collective-permute-done((bf16[64,7168]{1,0:T(8,128)(2,1)S(1)}, bf16[64,7168]{1,0:T(8,128)(2,1)S(1)}, u32[]{:S(2)}, u32[]{:S(2)}) %collective-permute-start.6) | collective-permute-done | bytes 917536 | tf_op jit(solution)/shard_map/ppermute | solution.py:71
  125.5 6.3 %collective-permute-done.7 = bf16[32,7168]{1,0:T(8,128)(2,1)S(1)} collective-permute-done((bf16[32,7168]{1,0:T(8,128)(2,1)S(1)}, bf16[32,7168]{1,0:T(8,128)(2,1)S(1)}, u32[]{:S(2)}, u32[]{:S(2)}) %collective-permute-start.7) | collective-permute-done | bytes 458784 | tf_op jit(solution)/shard_map/ppermute | solution.py:71
  133.2 6.4 %collective-permute-done.8 = bf16[16,7168]{1,0:T(8,128)(2,1)S(1)} collective-permute-done((bf16[16,7168]{1,0:T(8,128)(2,1)S(1)}, bf16[16,7168]{1,0:T(8,128)(2,1)S(1)}, u32[]{:S(2)}, u32[]{:S(2)}) %collective-permute-start.8) | collective-permute-done | bytes 229408 | tf_op jit(solution)/shard_map/ppermute | solution.py:71
  140.0 3.0 %collective-permute-start.25 = (bf16[8,7168]{1,0:T(8,128)(2,1)S(1)}, bf16[8,7168]{1,0:T(8,128)(2,1)S(1)}, u32[]{:S(2)}, u32[]{:S(2)}) collective-permute-start(bf16[8,7168]{1,0:T(8,128)(2,1)S(1)} %close.3), channel_id=1, source_target_pairs={{0,8},{1,9},{2,10},{3,11},{4,12},{5,13},{6,14},{7,15},{8,0},{9,1},... | collective-permute-start | bytes 344072 | tf_op jit(solution)/shard_map/ppermute | solution.py:71
  143.6 5.7 %collective-permute-done.9.came_ref = bf16[8,7168]{1,0:T(8,128)(2,1)S(1)} collective-permute-done((bf16[8,7168]{1,0:T(8,128)(2,1)S(1)}, bf16[8,7168]{1,0:T(8,128)(2,1)S(1)}, u32[]{:S(2)}, u32[]{:S(2)}) %collective-permute-start.9) | collective-permute-done | bytes 114720 | tf_op jit(solution)/shard_map/ppermute | solution.py:71
  152.4 3.8 %collective-permute-done.10 = bf16[8,7168]{1,0:T(8,128)(2,1)S(1)} collective-permute-done((bf16[8,7168]{1,0:T(8,128)(2,1)S(1)}, bf16[8,7168]{1,0:T(8,128)(2,1)S(1)}, u32[]{:S(2)}, u32[]{:S(2)}) %collective-permute-start.10) | collective-permute-done | bytes 114720 | tf_op jit(solution)/shard_map/ppermute | solution.py:71
  157.0 3.2 %collective-permute-done.26 = bf16[16,7168]{1,0:T(8,128)(2,1)S(1)} collective-permute-done((bf16[16,7168]{1,0:T(8,128)(2,1)S(1)}, bf16[16,7168]{1,0:T(8,128)(2,1)S(1)}, u32[]{:S(2)}, u32[]{:S(2)}) %collective-permute-start.26) | collective-permute-done | bytes 229408 | tf_op jit(solution)/shard_map/ppermute | solution.py:71
  160.2 2.3 collective-permute-start.27
  162.6 2.3 collective-permute-start.12
  165.7 6.6 %collective-permute-done.27 = bf16[32,7168]{1,0:T(8,128)(2,1)S(1)} collective-permute-done((bf16[32,7168]{1,0:T(8,128)(2,1)S(1)}, bf16[32,7168]{1,0:T(8,128)(2,1)S(1)}, u32[]{:S(2)}, u32[]{:S(2)}) %collective-permute-start.27) | collective-permute-done | bytes 458784 | tf_op jit(solution)/shard_map/ppermute | solution.py:71
  172.4 2.4 collective-permute-start.28
  174.7 7.4 %collective-permute-done.12 = bf16[32,7168]{1,0:T(8,128)(2,1)S(1)} collective-permute-done((bf16[32,7168]{1,0:T(8,128)(2,1)S(1)}, bf16[32,7168]{1,0:T(8,128)(2,1)S(1)}, u32[]{:S(2)}, u32[]{:S(2)}) %collective-permute-start.12) | collective-permute-done | bytes 458784 | tf_op jit(solution)/shard_map/ppermute | solution.py:71
  182.2 2.4 collective-permute-start.13
  187.2 8.8 %collective-permute-done.13 = bf16[64,7168]{1,0:T(8,128)(2,1)S(1)} collective-permute-done((bf16[64,7168]{1,0:T(8,128)(2,1)S(1)}, bf16[64,7168]{1,0:T(8,128)(2,1)S(1)}, u32[]{:S(2)}, u32[]{:S(2)}) %collective-permute-start.13) | collective-permute-done | bytes 917536 | tf_op jit(solution)/shard_map/ppermute | solution.py:71
  196.5 29.7 %head.3 = f32[32,16,128]{2,1,0:T(8,128)} custom-call(s32[32]{0:T(128)S(1)} %pad_add_fusion.owner_ref, bf16[128,7168]{1,0:T(8,128)(2,1)} %constant_dynamic-update-slice_fusion.15.near_ref, bf16[128,7168]{1,0:T(8,128)(2,1)} %collective-permute-done.29.far_ref, bf16[4040,7168]{1,0:T(8,128)(2,1)} %bitcast.26, s32[1,256]{1,0:T(1,128)S(1)} %squeeze.16.ids_ref, ...), custom_call_target="tpu_custom_call" | custom-call | flops 14826864640 | bytes 61587456 | tf_op jit(solution)/shard_map/head/pallas_call | solution.py:356
  226.1 4.2 %all-to-all-start.1 = ((f32[32,16,128]{2,1,0:T(8,128)}), f32[32,16,128]{2,1,0:T(8,128)S(1)}, u32[]{:S(2)}, u32[]{:S(2)}) async-start(f32[32,16,128]{2,1,0:T(8,128)} %head.3), calls=%async_computation.1 | async-start | bytes 524288 | tf_op jit(solution)/shard_map/all_to_all | solution.py:487
  230.3 13.8 %early_head.1.refs_0_ = f32[2040,256]{1,0:T(8,128)S(1)} custom-call(bf16[128,7168]{1,0:T(8,128)(2,1)S(1)} %constant_dynamic-update-slice_fusion.5.near_ref, bf16[128,7168]{1,0:T(8,128)(2,1)} %collective-permute-done.14.far_ref, bf16[4040,7168]{1,0:T(8,128)(2,1)} %bitcast.27), custom_call_target="tpu_custom_call" | custom-call | flops 7486832640 | bytes 32915456 | tf_op jit(solution)/shard_map/early_head/pallas_call | solution.py:232
  244.1 18.7 %head.2 = f32[32,16,128]{2,1,0:T(8,128)S(1)} custom-call(s32[32]{0:T(128)S(1)} %pad_add_fusion.owner_ref, bf16[128,7168]{1,0:T(8,128)(2,1)S(1)} %constant_dynamic-update-slice_fusion.5.near_ref, bf16[128,7168]{1,0:T(8,128)(2,1)} %collective-permute-done.14.far_ref, bf16[4040,7168]{1,0:T(8,128)(2,1)} %bitcast.28, s32[1,256]{1,0:T(1,128)S(1)} %squeeze.14.ids_ref, ...), custom_call_target="tpu_custom_call" | custom-call | flops 7340032000 | bytes 32342016 | tf_op jit(solution)/shard_map/head/pallas_call | solution.py:356
  262.8 16.9 %all_to_all.10.refs_0_ = f32[32,16,128]{2,1,0:T(8,128)} all-to-all(f32[32,16,128]{2,1,0:T(8,128)S(1)} %head.2), channel_id=1, replica_groups=mesh['section'=2,'vocab'=16] {'section','vocab'}, dimensions={0} | all-to-all | bytes 524288 | tf_op jit(solution)/shard_map/all_to_all | solution.py:487
  279.8 4.0 %finish.1 = (f32[2,128]{1,0:T(2,128)}, f32[2,128]{1,0:T(2,128)}, f32[2,128]{1,0:T(2,128)}, f32[2,128]{1,0:T(2,128)}) custom-call(f32[32,16,128]{2,1,0:T(8,128)} %all_to_all.10.refs_0_, f32[32,16,128]{2,1,0:T(8,128)} %copy-done.5), custom_call_target="tpu_custom_call" | custom-call | tf_op jit(solution)/shard_map/finish/pallas_call | solution.py:455
  (125 shorter events, 35.5 us)
Async XLA Ops:
  2.9 13.0 %collective-permute-start.15 = (bf16[8,7168]{1,0:T(8,128)(2,1)S(1)}, bf16[8,7168]{1,0:T(8,128)(2,1)S(1)}, u32[]{:S(2)}, u32[]{:S(2)}) collective-permute-start(bf16[8,7168]{1,0:T(8,128)(2,1)S(1)} %get-tuple-element.25), channel_id=1, source_target_pairs={{0,8},{1,9},{2,10},{3,11},{4,12},{5,13},{6,14},{7,15},{8,0},{9,1},... | collective-permute-start | bytes 344072 | tf_op jit(solution)/shard_map/ppermute | solution.py:71
  7.0 10.6 %collective-permute-start = (bf16[8,7168]{1,0:T(8,128)(2,1)S(1)}, bf16[8,7168]{1,0:T(8,128)(2,1)S(1)}, u32[]{:S(2)}, u32[]{:S(2)}) collective-permute-start(bf16[8,7168]{1,0:T(8,128)(2,1)S(1)} %get-tuple-element.29), channel_id=1, source_target_pairs={{0,8},{1,9},{2,10},{3,11},{4,12},{5,13},{6,14},{7,15},{8,0},{9,1},... | collective-permute-start | bytes 344072 | tf_op jit(solution)/shard_map/ppermute | solution.py:71
  16.0 8.5 %collective-permute-start.16 = (bf16[16,7168]{1,0:T(8,128)(2,1)S(1)}, bf16[16,7168]{1,0:T(8,128)(2,1)S(1)}, u32[]{:S(2)}, u32[]{:S(2)}) collective-permute-start(bf16[16,7168]{1,0:T(8,128)(2,1)S(1)} %pad_maximum_fusion.10), channel_id=1, source_target_pairs={{0,4},{1,5},{2,6},{3,7},{4,0},{5,1},{6,2},{7,3},{8,12},{9,13},{10,... | collective-permute-start | bytes 688136 | tf_op jit(solution)/shard_map/ppermute | solution.py:71
  17.6 9.8 %collective-permute-start.1 = (bf16[16,7168]{1,0:T(8,128)(2,1)S(1)}, bf16[16,7168]{1,0:T(8,128)(2,1)S(1)}, u32[]{:S(2)}, u32[]{:S(2)}) collective-permute-start(bf16[16,7168]{1,0:T(8,128)(2,1)S(1)} %pad_maximum_fusion.8), channel_id=1, source_target_pairs={{0,4},{1,5},{2,6},{3,7},{4,0},{5,1},{6,2},{7,3},{8,12},{9,13},{10,... | collective-permute-start | bytes 688136 | tf_op jit(solution)/shard_map/ppermute | solution.py:71
  24.5 10.9 %collective-permute-start.17 = (bf16[32,7168]{1,0:T(8,128)(2,1)S(1)}, bf16[32,7168]{1,0:T(8,128)(2,1)S(1)}, u32[]{:S(2)}, u32[]{:S(2)}) collective-permute-start(bf16[32,7168]{1,0:T(8,128)(2,1)S(1)} %pad_maximum_fusion.6), channel_id=1, source_target_pairs={{0,2},{1,3},{2,0},{3,1},{4,6},{5,7},{6,4},{7,5},{8,10},{9,11},{10,... | collective-permute-start | bytes 1376264 | tf_op jit(solution)/shard_map/ppermute | solution.py:71
  27.4 17.9 %collective-permute-start.2 = (bf16[32,7168]{1,0:T(8,128)(2,1)S(1)}, bf16[32,7168]{1,0:T(8,128)(2,1)S(1)}, u32[]{:S(2)}, u32[]{:S(2)}) collective-permute-start(bf16[32,7168]{1,0:T(8,128)(2,1)S(1)} %pad_maximum_fusion.4), channel_id=1, source_target_pairs={{0,2},{1,3},{2,0},{3,1},{4,6},{5,7},{6,4},{7,5},{8,10},{9,11},{10,... | collective-permute-start | bytes 1376264 | tf_op jit(solution)/shard_map/ppermute | solution.py:71
  35.6 13.8 %collective-permute-start.18 = (bf16[64,7168]{1,0:T(8,128)(2,1)S(1)}, bf16[64,7168]{1,0:T(8,128)(2,1)S(1)}, u32[]{:S(2)}, u32[]{:S(2)}) collective-permute-start(bf16[64,7168]{1,0:T(8,128)(2,1)S(1)} %pad_maximum_fusion.2), channel_id=1, source_target_pairs={{0,1},{1,0},{2,3},{3,2},{4,5},{5,4},{6,7},{7,6},{8,9},{9,8},{10,11... | collective-permute-start | bytes 2752520 | tf_op jit(solution)/shard_map/ppermute | solution.py:71
  45.4 13.8 %collective-permute-start.3 = (bf16[64,7168]{1,0:T(8,128)(2,1)S(1)}, bf16[64,7168]{1,0:T(8,128)(2,1)S(1)}, u32[]{:S(2)}, u32[]{:S(2)}) collective-permute-start(bf16[64,7168]{1,0:T(8,128)(2,1)S(1)} %pad_maximum_fusion), channel_id=1, source_target_pairs={{0,1},{1,0},{2,3},{3,2},{4,5},{5,4},{6,7},{7,6},{8,9},{9,8},{10,11... | collective-permute-start | bytes 2752520 | tf_op jit(solution)/shard_map/ppermute | solution.py:71
  49.4 9.9 %collective-permute-start.19 = (bf16[128,7168]{1,0:T(8,128)(2,1)S(1)}, bf16[128,7168]{1,0:T(8,128)(2,1)S(1)}, u32[]{:S(2)}, u32[]{:S(2)}) collective-permute-start(bf16[128,7168]{1,0:T(8,128)(2,1)S(1)} %constant_dynamic-update-slice_fusion.10.near_ref), channel_id=1, source_target_pairs={{0,16},{1,17},{2,18},{3,19},{4,20},{5,21},{6,22},{7,23},{8,24},{9,... | collective-permute-start | bytes 5505032 | tf_op jit(solution)/shard_map/ppermute | solution.py:71
  59.2 15.9 %collective-permute-start.4 = (bf16[128,7168]{1,0:T(8,128)(2,1)S(1)}, bf16[128,7168]{1,0:T(8,128)(2,1)S(1)}, u32[]{:S(2)}, u32[]{:S(2)}) collective-permute-start(bf16[128,7168]{1,0:T(8,128)(2,1)S(1)} %constant_dynamic-update-slice_fusion.near_ref), channel_id=1, source_target_pairs={{0,16},{1,17},{2,18},{3,19},{4,20},{5,21},{6,22},{7,23},{8,24},{9,... | collective-permute-start | bytes 5505032 | tf_op jit(solution)/shard_map/ppermute | solution.py:71
  74.6 16.4 %collective-permute-start.20 = (bf16[128,7168]{1,0:T(8,128)(2,1)}, bf16[128,7168]{1,0:T(8,128)(2,1)}, u32[]{:S(2)}, u32[]{:S(2)}) collective-permute-start(bf16[128,7168]{1,0:T(8,128)(2,1)} %get-tuple-element.15), channel_id=1, source_target_pairs={{0,16},{1,17},{2,18},{3,19},{4,20},{5,21},{6,22},{7,23},{8,24},{9,... | collective-permute-start | bytes 5505032 | tf_op jit(solution)/shard_map/ppermute | solution.py:71
  90.5 7.6 %collective-permute-start.5 = (bf16[128,7168]{1,0:T(8,128)(2,1)}, bf16[128,7168]{1,0:T(8,128)(2,1)}, u32[]{:S(2)}, u32[]{:S(2)}) collective-permute-start(bf16[128,7168]{1,0:T(8,128)(2,1)} %get-tuple-element.13), channel_id=1, source_target_pairs={{0,16},{1,17},{2,18},{3,19},{4,20},{5,21},{6,22},{7,23},{8,24},{9,... | collective-permute-start | bytes 5505032 | tf_op jit(solution)/shard_map/ppermute | solution.py:71
  94.8 13.6 %collective-permute-start.21 = (bf16[64,7168]{1,0:T(8,128)(2,1)S(1)}, bf16[64,7168]{1,0:T(8,128)(2,1)}, u32[]{:S(2)}, u32[]{:S(2)}) collective-permute-start(bf16[64,7168]{1,0:T(8,128)(2,1)S(1)} %slice.121), channel_id=1, source_target_pairs={{0,1},{1,0},{2,3},{3,2},{4,5},{5,4},{6,7},{7,6},{8,9},{9,8},{10,11... | collective-permute-start | bytes 2752520 | tf_op jit(solution)/shard_map/ppermute | solution.py:71
  100.1 22.9 %collective-permute-start.6 = (bf16[64,7168]{1,0:T(8,128)(2,1)S(1)}, bf16[64,7168]{1,0:T(8,128)(2,1)S(1)}, u32[]{:S(2)}, u32[]{:S(2)}) collective-permute-start(bf16[64,7168]{1,0:T(8,128)(2,1)S(1)} %slice.111), channel_id=1, source_target_pairs={{0,1},{1,0},{2,3},{3,2},{4,5},{5,4},{6,7},{7,6},{8,9},{9,8},{10,11... | collective-permute-start | bytes 2752520 | tf_op jit(solution)/shard_map/ppermute | solution.py:71
  109.7 15.6 %collective-permute-start.22 = (bf16[32,7168]{1,0:T(8,128)(2,1)S(1)}, bf16[32,7168]{1,0:T(8,128)(2,1)S(1)}, u32[]{:S(2)}, u32[]{:S(2)}) collective-permute-start(bf16[32,7168]{1,0:T(8,128)(2,1)S(1)} %slice.123), channel_id=1, source_target_pairs={{0,2},{1,3},{2,0},{3,1},{4,6},{5,7},{6,4},{7,5},{8,10},{9,11},{10,... | collective-permute-start | bytes 1376264 | tf_op jit(solution)/shard_map/ppermute | solution.py:71
  123.2 8.6 %collective-permute-start.7 = (bf16[32,7168]{1,0:T(8,128)(2,1)S(1)}, bf16[32,7168]{1,0:T(8,128)(2,1)S(1)}, u32[]{:S(2)}, u32[]{:S(2)}) collective-permute-start(bf16[32,7168]{1,0:T(8,128)(2,1)S(1)} %slice.113), channel_id=1, source_target_pairs={{0,2},{1,3},{2,0},{3,1},{4,6},{5,7},{6,4},{7,5},{8,10},{9,11},{10,... | collective-permute-start | bytes 1376264 | tf_op jit(solution)/shard_map/ppermute | solution.py:71
  125.4 6.5 %collective-permute-start.23 = (bf16[16,7168]{1,0:T(8,128)(2,1)S(1)}, bf16[16,7168]{1,0:T(8,128)(2,1)S(1)}, u32[]{:S(2)}, u32[]{:S(2)}) collective-permute-start(bf16[16,7168]{1,0:T(8,128)(2,1)S(1)} %slice.125), channel_id=1, source_target_pairs={{0,4},{1,5},{2,6},{3,7},{4,0},{5,1},{6,2},{7,3},{8,12},{9,13},{10,... | collective-permute-start | bytes 688136 | tf_op jit(solution)/shard_map/ppermute | solution.py:71
  131.8 7.8 %collective-permute-start.8 = (bf16[16,7168]{1,0:T(8,128)(2,1)S(1)}, bf16[16,7168]{1,0:T(8,128)(2,1)S(1)}, u32[]{:S(2)}, u32[]{:S(2)}) collective-permute-start(bf16[16,7168]{1,0:T(8,128)(2,1)S(1)} %slice.115), channel_id=1, source_target_pairs={{0,4},{1,5},{2,6},{3,7},{4,0},{5,1},{6,2},{7,3},{8,12},{9,13},{10,... | collective-permute-start | bytes 688136 | tf_op jit(solution)/shard_map/ppermute | solution.py:71
  132.0 7.8 %collective-permute-start.24 = (bf16[8,7168]{1,0:T(8,128)(2,1)S(1)}, bf16[8,7168]{1,0:T(8,128)(2,1)S(1)}, u32[]{:S(2)}, u32[]{:S(2)}) collective-permute-start(bf16[8,7168]{1,0:T(8,128)(2,1)S(1)} %get-tuple-element.30), channel_id=1, source_target_pairs={{0,8},{1,9},{2,10},{3,11},{4,12},{5,13},{6,14},{7,15},{8,0},{9,1},... | collective-permute-start | bytes 344072 | tf_op jit(solution)/shard_map/ppermute | solution.py:71
  139.7 9.7 %collective-permute-start.9 = (bf16[8,7168]{1,0:T(8,128)(2,1)S(1)}, bf16[8,7168]{1,0:T(8,128)(2,1)S(1)}, u32[]{:S(2)}, u32[]{:S(2)}) collective-permute-start(bf16[8,7168]{1,0:T(8,128)(2,1)S(1)} %get-tuple-element.32), channel_id=1, source_target_pairs={{0,8},{1,9},{2,10},{3,11},{4,12},{5,13},{6,14},{7,15},{8,0},{9,1},... | collective-permute-start | bytes 344072 | tf_op jit(solution)/shard_map/ppermute | solution.py:71
  140.0 11.6 %collective-permute-start.25 = (bf16[8,7168]{1,0:T(8,128)(2,1)S(1)}, bf16[8,7168]{1,0:T(8,128)(2,1)S(1)}, u32[]{:S(2)}, u32[]{:S(2)}) collective-permute-start(bf16[8,7168]{1,0:T(8,128)(2,1)S(1)} %close.3), channel_id=1, source_target_pairs={{0,8},{1,9},{2,10},{3,11},{4,12},{5,13},{6,14},{7,15},{8,0},{9,1},... | collective-permute-start | bytes 344072 | tf_op jit(solution)/shard_map/ppermute | solution.py:71
  149.5 6.7 %collective-permute-start.10 = (bf16[8,7168]{1,0:T(8,128)(2,1)S(1)}, bf16[8,7168]{1,0:T(8,128)(2,1)S(1)}, u32[]{:S(2)}, u32[]{:S(2)}) collective-permute-start(bf16[8,7168]{1,0:T(8,128)(2,1)S(1)} %close.2), channel_id=1, source_target_pairs={{0,8},{1,9},{2,10},{3,11},{4,12},{5,13},{6,14},{7,15},{8,0},{9,1},... | collective-permute-start | bytes 344072 | tf_op jit(solution)/shard_map/ppermute | solution.py:71
  151.6 8.5 %collective-permute-start.26 = (bf16[16,7168]{1,0:T(8,128)(2,1)S(1)}, bf16[16,7168]{1,0:T(8,128)(2,1)S(1)}, u32[]{:S(2)}, u32[]{:S(2)}) collective-permute-start(bf16[16,7168]{1,0:T(8,128)(2,1)S(1)} %pad_maximum_fusion.11), channel_id=1, source_target_pairs={{0,4},{1,5},{2,6},{3,7},{4,0},{5,1},{6,2},{7,3},{8,12},{9,13},{10,... | collective-permute-start | bytes 688136 | tf_op jit(solution)/shard_map/ppermute | solution.py:71
  156.2 6.4 %collective-permute-start.11 = (bf16[16,7168]{1,0:T(8,128)(2,1)S(1)}, bf16[16,7168]{1,0:T(8,128)(2,1)S(1)}, u32[]{:S(2)}, u32[]{:S(2)}) collective-permute-start(bf16[16,7168]{1,0:T(8,128)(2,1)S(1)} %pad_maximum_fusion.9), channel_id=1, source_target_pairs={{0,4},{1,5},{2,6},{3,7},{4,0},{5,1},{6,2},{7,3},{8,12},{9,13},{10,... | collective-permute-start | bytes 688136 | tf_op jit(solution)/shard_map/ppermute | solution.py:71
  160.2 12.1 %collective-permute-start.27 = (bf16[32,7168]{1,0:T(8,128)(2,1)S(1)}, bf16[32,7168]{1,0:T(8,128)(2,1)S(1)}, u32[]{:S(2)}, u32[]{:S(2)}) collective-permute-start(bf16[32,7168]{1,0:T(8,128)(2,1)S(1)} %pad_maximum_fusion.7), channel_id=1, source_target_pairs={{0,2},{1,3},{2,0},{3,1},{4,6},{5,7},{6,4},{7,5},{8,10},{9,11},{10,... | collective-permute-start | bytes 1376264 | tf_op jit(solution)/shard_map/ppermute | solution.py:71
  162.6 19.5 %collective-permute-start.12 = (bf16[32,7168]{1,0:T(8,128)(2,1)S(1)}, bf16[32,7168]{1,0:T(8,128)(2,1)S(1)}, u32[]{:S(2)}, u32[]{:S(2)}) collective-permute-start(bf16[32,7168]{1,0:T(8,128)(2,1)S(1)} %pad_maximum_fusion.5), channel_id=1, source_target_pairs={{0,2},{1,3},{2,0},{3,1},{4,6},{5,7},{6,4},{7,5},{8,10},{9,11},{10,... | collective-permute-start | bytes 1376264 | tf_op jit(solution)/shard_map/ppermute | solution.py:71
  172.4 13.7 %collective-permute-start.28 = (bf16[64,7168]{1,0:T(8,128)(2,1)S(1)}, bf16[64,7168]{1,0:T(8,128)(2,1)S(1)}, u32[]{:S(2)}, u32[]{:S(2)}) collective-permute-start(bf16[64,7168]{1,0:T(8,128)(2,1)S(1)} %pad_maximum_fusion.3), channel_id=1, source_target_pairs={{0,1},{1,0},{2,3},{3,2},{4,5},{5,4},{6,7},{7,6},{8,9},{9,8},{10,11... | collective-permute-start | bytes 2752520 | tf_op jit(solution)/shard_map/ppermute | solution.py:71
  182.2 13.7 %collective-permute-start.13 = (bf16[64,7168]{1,0:T(8,128)(2,1)S(1)}, bf16[64,7168]{1,0:T(8,128)(2,1)S(1)}, u32[]{:S(2)}, u32[]{:S(2)}) collective-permute-start(bf16[64,7168]{1,0:T(8,128)(2,1)S(1)} %pad_maximum_fusion.1), channel_id=1, source_target_pairs={{0,1},{1,0},{2,3},{3,2},{4,5},{5,4},{6,7},{7,6},{8,9},{9,8},{10,11... | collective-permute-start | bytes 2752520 | tf_op jit(solution)/shard_map/ppermute | solution.py:71
  187.1 9.3 %collective-permute-start.29 = (bf16[128,7168]{1,0:T(8,128)(2,1)}, bf16[128,7168]{1,0:T(8,128)(2,1)}, u32[]{:S(2)}, u32[]{:S(2)}) collective-permute-start(bf16[128,7168]{1,0:T(8,128)(2,1)} %constant_dynamic-update-slice_fusion.15.near_ref), channel_id=1, source_target_pairs={{0,16},{1,17},{2,18},{3,19},{4,20},{5,21},{6,22},{7,23},{8,24},{9,... | collective-permute-start | bytes 5505032 | tf_op jit(solution)/shard_map/ppermute | solution.py:71
  196.0 34.3 %collective-permute-start.14 = (bf16[128,7168]{1,0:T(8,128)(2,1)S(1)}, bf16[128,7168]{1,0:T(8,128)(2,1)}, u32[]{:S(2)}, u32[]{:S(2)}) collective-permute-start(bf16[128,7168]{1,0:T(8,128)(2,1)S(1)} %constant_dynamic-update-slice_fusion.5.near_ref), channel_id=1, source_target_pairs={{0,16},{1,17},{2,18},{3,19},{4,20},{5,21},{6,22},{7,23},{8,24},{9,... | collective-permute-start | bytes 5505032 | tf_op jit(solution)/shard_map/ppermute | solution.py:71
  226.1 36.7 %all-to-all-start.1 = ((f32[32,16,128]{2,1,0:T(8,128)}), f32[32,16,128]{2,1,0:T(8,128)S(1)}, u32[]{:S(2)}, u32[]{:S(2)}) async-start(f32[32,16,128]{2,1,0:T(8,128)} %head.3), calls=%async_computation.1 | async-start | bytes 524288 | tf_op jit(solution)/shard_map/all_to_all | solution.py:487
  262.8 16.9 %copy-start.5 = (f32[32,16,128]{2,1,0:T(8,128)}, f32[32,16,128]{2,1,0:T(8,128)S(1)}, u32[]{:S(2)}) copy-start(f32[32,16,128]{2,1,0:T(8,128)S(1)} %all-to-all-done.1.refs_1_) | copy-start | bytes 786436
  (9 other events, 64.1 us)
